TPU v7x, 32 devices: a whole 2x2x4 slice. The times are simulated.
32 devices in a mesh: rows: 16 (over z, y, x), cols: 2 (over core).
Axes of the slice: x: 2, y: 2, z: 4, core: 2. Of those that a mesh axis runs over, the one named last changes fastest.
Arguments:
- design: float32 [16384, 512], P('rows', 'cols'), may hold values from -24 to 24
- signs: int32 [16384], P('rows'), may hold values from -1 to 1, as said below
- kept: int32 [1024], replicated, may hold values from 0 to 16383, as said below
Outputs:
- sketch: float32 [1024, 512], P('rows', 'cols')
- factor: float32 [512, 512], P(None, 'cols')
Inputs may be any that keep to these rules, and one draw needn't show every extreme that they name: `signs`: each entry is +1 or -1. `kept`: distinct and increasing.
All inputs are finite; a program needn't handle non-finite values.
Results may differ from a plain program's by a relative error of at most 0.0003.
Values sent between devices are 32-bit elements; how exact they have to be, the bound alone decides.
A program may use at most 64 MiB of HBM per device.

v0:
```python
import math

import jax
import jax.numpy as jnp
from jax import lax
from jax.sharding import PartitionSpec as P


def hadamard(order):
    matrix = jnp.ones((1, 1), jnp.float32)
    base = jnp.array([[1.0, 1.0], [1.0, -1.0]], jnp.float32)
    while matrix.shape[0] < order:
        matrix = jnp.kron(matrix, base)
    return matrix


def bit_parity(value):
    folded = value
    for amount in (16, 8, 4, 2, 1):
        folded = jnp.bitwise_xor(folded, jnp.right_shift(folded, amount))
    return jnp.bitwise_and(folded, 1)


def local_transform(flipped):
    length, width = flipped.shape
    outer = length // 128
    inner_table = hadamard(128)
    outer_table = hadamard(outer)
    blocks = flipped.reshape(outer, 128, width)
    mixed = jnp.einsum("pb,abc->apc", inner_table, blocks, precision=lax.Precision.HIGHEST)
    mixed = jnp.einsum("qa,apc->qpc", outer_table, mixed, precision=lax.Precision.HIGHEST)
    return mixed.reshape(length, width)


def signed_rows(transformed, kept_part, device_row, total_rows):
    length = transformed.shape[0]
    kept_blocks = kept_part // length
    offsets = kept_part - kept_blocks * length
    parity = bit_parity(jnp.bitwise_and(kept_blocks, device_row))
    factor = (1.0 - 2.0 * parity.astype(jnp.float32)) / math.sqrt(total_rows)
    return jnp.take(transformed, offsets, axis=0) * factor[:, None]


def source_total(received):
    return jnp.sum(received, axis=0)


def body(design, signs, kept):
    flipped = design * signs.astype(jnp.float32)[:, None]
    transformed = local_transform(flipped)
    device_row = lax.axis_index("rows")
    groups = lax.axis_size("rows")
    length = transformed.shape[0]
    widths = transformed.shape[1]
    total_rows = length * groups
    per_device = kept.shape[0] // groups
    outgoing = signed_rows(transformed, kept, device_row, total_rows)
    outgoing = outgoing.reshape(groups, per_device, widths)
    sketch = source_total(lax.all_to_all(outgoing, "rows", split_axis=0, concat_axis=0, tiled=True))
    column = lax.axis_index("cols")
    whole = lax.all_gather(sketch, "cols", axis=1, tiled=True)
    kept_total = kept.shape[0]
    partial_gram = jnp.dot(
        whole.T, whole, precision=lax.Precision.HIGHEST, preferred_element_type=jnp.float32
    )
    gram = lax.psum(partial_gram, "rows") / kept_total
    factor = jnp.linalg.cholesky(gram).T
    return (sketch, lax.dynamic_slice_in_dim(factor, column * widths, widths, 1))


def solution(mesh):
    placed = (P("rows", "cols"), P("rows"), P())
    return jax.shard_map(
        body,
        mesh=mesh,
        in_specs=placed,
        out_specs=(P("rows", "cols"), P(None, "cols")),
        check_vma=False,
    )
```

profile of v0, /device:TPU:0, one launch (start us, length us, event | category | flops | bytes accessed | tf_op | source)
XLA Modules:
  0.0 271.5 jit_solution(705625595434788475)
XLA Ops:
  7.2 0.8 broadcast_multiply_fusion.7
  8.1 0.8 broadcast_multiply_fusion.6
  10.4 0.8 broadcast_multiply_fusion.5
  11.3 0.8 broadcast_multiply_fusion.4
  12.2 0.9 broadcast_multiply_fusion.2
  13.8 3.1 %broadcast_multiply_fusion = f32[64,2,64,2]{3,2,1,0:T(8,128)} fusion(f32[2,2]{1,0:T(2,128)} %constant.202.clone, f32[64,64]{1,0:T(8,128)S(1)} %mul.278), kind=kLoop, calls=%fused_computation.1 | loop fusion | flops 16384 | bytes 81936 | tf_op jit(solution)/shard_map/jit(kron)/mul | solution.py:13
  16.9 4.0 %reshape.202 = f32[128,128,1]{1,0,2:T(8,128)S(1)} reshape(f32[64,2,64,2]{3,2,1,0:T(8,128)} %broadcast_multiply_fusion) | data formatting | bytes 131072 | tf_op jit(solution)/shard_map/jit(kron)/mul | solution.py:13
  21.1 1.8 fusion.23
  23.4 1.0 fusion.1
  25.0 3.5 %gather_fusion = f32[1024,256]{1,0:T(8,128)S(1)} fusion(f32[1024,256]{1,0:T(8,128)S(1)} %bitcast.43, s32[1024]{0:T(1024)S(1)} %broadcast_clamp_fusion), kind=kCustom, calls=%fused_computation | custom fusion | bytes 2101248 | tf_op jit(solution)/shard_map/jit(_take)/gather | solution.py:41
  28.8 34.5 %all_to_all.5 = f32[16,64,256]{2,1,0:T(8,128)S(1)} all-to-all(f32[16,64,256]{2,1,0:T(8,128)S(1)} %select_multiply_fusion), channel_id=1, replica_groups=mesh['rows'=16,'cols'=2] {'rows'}, dimensions={0} | all-to-all | bytes 2097152 | tf_op jit(solution)/shard_map/all_to_all | solution.py:59
  63.3 2.1 all_gather.3
  65.4 2.1 fusion.24
  67.5 110.9 %all-reduce.3.cloned.1.call-done = f32[512,512]{0,1:T(8,128)} async-done(((f32[512,512]{0,1:T(8,128)}), f32[512,512]{0,1:T(8,128)}) %all-reduce.3.cloned.1.call-update) | async-done | bytes 1048592 | tf_op jit(solution)/shard_map/psum | solution.py:66
  178.4 1.4 broadcast_multiply_fusion.1
  180.4 11.7 %cholesky.104 = f32[128,128]{1,0:T(8,128)S(1)} custom-call(f32[128,128]{1,0:T(8,128)S(1)} %cholesky.266), custom_call_target="Cholesky" | custom-call | tf_op jit(solution)/shard_map/jit(cholesky)/cholesky | solution.py:67
  192.3 9.8 %custom-call.27 = f32[1,128,128]{1,2,0:T(8,128)S(1)} custom-call(f32[1,128,128]{2,1,0:T(8,128)S(1)} %get-tuple-element.15), custom_call_target="InvertDiagBlocksLowerTriangular" | custom-call | tf_op jit(solution)/shard_map/jit(cholesky)/cholesky | solution.py:67
  202.7 11.7 %cholesky.217 = f32[128,128]{1,0:T(8,128)S(1)} custom-call(f32[128,128]{1,0:T(8,128)S(1)} %cholesky.270), custom_call_target="Cholesky" | custom-call | tf_op jit(solution)/shard_map/jit(cholesky)/cholesky | solution.py:67
  214.5 9.9 %custom-call.28 = f32[1,128,128]{1,2,0:T(8,128)S(1)} custom-call(f32[1,128,128]{2,1,0:T(8,128)S(1)} %get-tuple-element.12), custom_call_target="InvertDiagBlocksLowerTriangular" | custom-call | tf_op jit(solution)/shard_map/jit(cholesky)/cholesky | solution.py:67
  225.1 11.7 %cholesky.238 = f32[128,128]{1,0:T(8,128)S(1)} custom-call(f32[128,128]{1,0:T(8,128)S(1)} %cholesky.275), custom_call_target="Cholesky" | custom-call | tf_op jit(solution)/shard_map/jit(cholesky)/cholesky | solution.py:67
  236.8 0.7 compare_reduce_fusion.1
  237.6 9.8 %custom-call.29 = f32[1,128,128]{1,2,0:T(8,128)S(1)} custom-call(f32[1,128,128]{2,1,0:T(8,128)S(1)} %get-tuple-element.9), custom_call_target="InvertDiagBlocksLowerTriangular" | custom-call | tf_op jit(solution)/shard_map/jit(cholesky)/cholesky | solution.py:67
  248.0 11.7 %cholesky.255 = f32[128,128]{1,0:T(8,128)S(1)} custom-call(f32[128,128]{1,0:T(8,128)S(1)} %convolution_subtract_fusion.2), custom_call_target="Cholesky" | custom-call | tf_op jit(solution)/shard_map/jit(cholesky)/cholesky | solution.py:67
  263.6 1.0 copy.13
  (48 shorter events, 8.3 us)
Async XLA Ops:
  7.2 171.2 %all-reduce.3.cloned.1.call-start = ((), (), s32[]{:S(2)}) async-start(), calls=%async_computation.1 | async-start | bytes 2097152 | tf_op jit(solution)/shard_map/psum | solution.py:66
  13.8 7.1 %copy-start.4 = (s32[1024]{0:T(1024)S(1)}, s32[1024]{0:T(1024)}, u32[]{:S(2)}) copy-start(s32[1024]{0:T(1024)} %param.6) | copy-start | bytes 12292
  13.8 7.1 %copy-start.1 = (f32[1024,256]{1,0:T(8,128)S(1)}, f32[1024,256]{1,0:T(8,128)}, u32[]{:S(2)}) copy-start(f32[1024,256]{1,0:T(8,128)} %param.5) | copy-start | bytes 3145732
  21.1 3.6 %copy-start.3 = (s32[1024]{0:T(1024)S(1)}, s32[1024]{0:T(1024)}, u32[]{:S(2)}) copy-start(s32[1024]{0:T(1024)} %param.7) | copy-start | bytes 12292
  63.3 117.1 %copy-start.2 = (f32[64,256]{1,0:T(8,128)}, f32[64,256]{1,0:T(8,128)S(1)}, u32[]{:S(2)}) copy-start(f32[64,256]{1,0:T(8,128)S(1)} %reduce_sum.9) | copy-start | bytes 196612
  178.3 1.8 copy-start
Sparse Core Ops, SparseCore 0:
  67.6 110.7 all-reduce.2
where the time goes:
time: 272 us; the launch traced here: 271 us
  waiting for transfers between devices  111 us (41%)
  other arithmetic  89.4 us (33%)
  blocking collectives  36.5 us (13%)
  between operations  16.9 us (6%)
  local copies, waits for them, and re-layouts  11 us (4%)
  matrix products  6.7 us (2%)
    psum x1, waiting for transfers between devices, body(): gram = lax.psum(partial_gram, 'rows') / kept_total  111 us
    another operation x14, other arithmetic, body(): factor = jnp.linalg.cholesky(gram).T  78.6 us
    all_to_all x1, blocking collectives, body(): lax.all_to_all(outgoing, 'rows', split_axis=0, concat_axis=0, tiled=True)  34.5 us
    mul x6, other arithmetic, hadamard(): matrix = jnp.kron(matrix, base)  7.1 us
  transfers between devices with their start and end apart: 1, of which 1 were waited for; matrix products, arithmetic and copies ran while one was open for 0% of the time, Pallas kernels for 0%

commit v1 on v0

v1 whole, which is shorter than its diff:
```python
import functools
import math

import jax
import jax.numpy as jnp
from jax import lax
from jax.experimental import pallas as pl
from jax.experimental.pallas import tpu as pltpu
from jax.sharding import PartitionSpec as P

MESH = pl.DeviceIdType.MESH
HIGHEST = lax.Precision.HIGHEST
LANES = 128


def transform_kernel(scale, tile, design_ref, signs_ref, kept_ref, out_ref, split):
    length = design_ref.shape[0]
    values = design_ref[...]
    high = values.astype(jnp.bfloat16)
    rest = values - high.astype(jnp.float32)
    middle = rest.astype(jnp.bfloat16)
    split[0] = high
    split[1] = middle
    split[2] = (rest - middle.astype(jnp.float32)).astype(jnp.bfloat16)
    first_row = lax.axis_index("rows") * length
    lane = lax.broadcasted_iota(jnp.int32, (LANES, LANES), 1)

    def step(index, carry):
        stacked = []
        for piece in range(tile // LANES):
            row = kept_ref[pl.ds(index * (tile // LANES) + piece, 1), :]
            column = jnp.broadcast_to(row, (LANES, LANES)).T
            blocks = []
            for block in range(length // LANES):
                common = jnp.bitwise_and(column, lane + (first_row + block * LANES))
                odd = jnp.bitwise_and(lax.population_count(common), 1)
                flips = signs_ref[block : block + 1, :]
                entry = (1 - 2 * odd) * flips
                blocks.append(entry.astype(jnp.float32).astype(jnp.bfloat16))
            stacked.append(jnp.concatenate(blocks, axis=1))
        table = jnp.concatenate(stacked, axis=0)
        total = jnp.dot(table, split[2], preferred_element_type=jnp.float32)
        total += jnp.dot(table, split[1], preferred_element_type=jnp.float32)
        total += jnp.dot(table, split[0], preferred_element_type=jnp.float32)
        out_ref[pl.ds(pl.multiple_of(index * tile, tile), tile), :] = total * scale
        return carry

    lax.fori_loop(0, out_ref.shape[0] // tile, step, 0)


def transform(design, signs, kept, total_rows):
    length, width = design.shape
    count = kept.shape[0]
    tile = 256
    return pl.pallas_call(
        functools.partial(transform_kernel, 1.0 / math.sqrt(total_rows), tile),
        out_shape=jax.ShapeDtypeStruct((count, width), jnp.float32),
        in_specs=[pl.BlockSpec(memory_space=pltpu.VMEM)] * 3,
        out_specs=pl.BlockSpec(memory_space=pltpu.VMEM),
        scratch_shapes=[pltpu.VMEM((3, length, width), jnp.bfloat16)],
        cost_estimate=pl.CostEstimate(
            flops=6 * count * length * width, bytes_accessed=4 * (count + length) * width, transcendentals=0
        ),
    )(design, signs.reshape(-1, LANES), kept.reshape(-1, LANES))


def exchange_kernel(
    n, orders, x_ref, sketch_ref, gram_ref, buf, recv, gat,
    rs_send, rs_recv, ag_send, ag_recv, ex_send, ex_recv,
):
    me = lax.axis_index("rows")
    core = lax.axis_index("cols")
    levels = len(orders[0])
    parts = len(orders)
    width = x_ref.shape[2]
    sub = x_ref.shape[1] // parts

    def flip(bit):
        return (1 - 2 * ((me // (1 << bit)) % 2)) * (1 << bit)

    barrier = pltpu.get_barrier_semaphore()
    for bit in range(levels):
        pl.semaphore_signal(barrier, inc=1, device_id=(me + flip(bit), core), device_id_type=MESH)
    pl.semaphore_signal(barrier, inc=1, device_id=(me, 1 - core), device_id_type=MESH)

    def slot_owner(part, slot):
        owner = me
        for place, bit in enumerate(orders[part]):
            if (slot >> (levels - 1 - place)) & 1:
                owner = owner + flip(bit)
        return owner

    lanes = pl.ds(pl.multiple_of(core * width, LANES), width)

    for part in range(parts):
        for slot in range(n - 1, -1, -1):
            buf[part, slot] = x_ref[slot_owner(part, slot), part * sub : (part + 1) * sub, :]
    pl.semaphore_wait(barrier, levels + 1)

    def reduce_copy(part, level):
        half = n >> (level + 1)
        return pltpu.make_async_remote_copy(
            src_ref=buf.at[part, pl.ds(half, half)],
            dst_ref=recv.at[part, pl.ds(half, half)],
            send_sem=rs_send.at[part, level],
            recv_sem=rs_recv.at[part, level],
            device_id=(me + flip(orders[part][level]), core),
            device_id_type=MESH,
        )

    for part in range(parts):
        reduce_copy(part, 0).start()
    for level in range(levels):
        half = n >> (level + 1)
        for part in range(parts):
            reduce_copy(part, level).wait_recv()
            if level + 1 < levels:
                low = half // 2
                buf[part, low:half] += recv[part, half + low : 2 * half]
                reduce_copy(part, level + 1).start()
                buf[part, 0:low] += recv[part, half : half + low]
            else:
                own = buf[part, 0] + recv[part, 1]
                sketch_ref[part * sub : (part + 1) * sub, :] = own
                gat[part, 0, :, lanes] = own

    def gather_copy(part, level):
        half = n >> (level + 1)
        return pltpu.make_async_remote_copy(
            src_ref=gat.at[part, pl.ds(0, half), :, lanes],
            dst_ref=gat.at[part, pl.ds(half, half), :, lanes],
            send_sem=ag_send.at[part, level],
            recv_sem=ag_recv.at[part, level],
            device_id=(me + flip(orders[part][level]), core),
            device_id_type=MESH,
        )

    def core_copy(part, level):
        start, size = (0, 1) if level == levels else (n >> (level + 1), n >> (level + 1))
        return pltpu.make_async_remote_copy(
            src_ref=gat.at[part, pl.ds(start, size), :, lanes],
            dst_ref=gat.at[part, pl.ds(start, size), :, lanes],
            send_sem=ex_send.at[part, level],
            recv_sem=ex_recv.at[part, level],
            device_id=(me, 1 - core),
            device_id_type=MESH,
        )

    def add_gram(start, size, first):
        whole = gat.shape[3]
        half = whole // 2
        group = min(size, 8)
        if first:
            gram_ref[...] = jnp.zeros_like(gram_ref)

        def step(index, carry):
            part, piece = index // (size // group), index % (size // group)
            rows = gat[part, pl.ds(start + piece * group, group)].reshape(group * sub, whole)
            dims = (((0,), (0,)), ((), ()))
            gram_ref[0:half, :] += lax.dot_general(
                rows[:, :half], rows, dims, precision=HIGHEST, preferred_element_type=jnp.float32
            )
            gram_ref[half:, half:] += lax.dot_general(
                rows[:, half:], rows[:, half:], dims, precision=HIGHEST, preferred_element_type=jnp.float32
            )
            return carry

        lax.fori_loop(0, parts * (size // group), step, 0)

    for part in range(parts):
        gather_copy(part, levels - 1).start()
        core_copy(part, levels).start()
    for level in range(levels - 1, 0, -1):
        for part in range(parts):
            gather_copy(part, level).wait_recv()
            gather_copy(part, level - 1).start()
            core_copy(part, level).start()
    for level in range(levels, 0, -1):
        for part in range(parts):
            core_copy(part, level).wait_recv()
    add_gram(0, n // 2, True)
    for part in range(parts):
        gather_copy(part, 0).wait_recv()
        core_copy(part, 0).start()
    for part in range(parts):
        core_copy(part, 0).wait_recv()
    add_gram(n // 2, n // 2, False)
    for part in range(parts):
        for level in range(levels):
            reduce_copy(part, level).wait_send()
            gather_copy(part, level).wait_send()
        for level in range(levels + 1):
            core_copy(part, level).wait_send()


def exchange(outgoing, n, cores):
    count, width = outgoing.shape
    per = count // n
    levels = n.bit_length() - 1
    parts = 2
    orders = []
    for part in range(parts):
        order = list(range(levels))
        if part % 2 and levels > 1:
            order[0], order[1] = order[1], order[0]
        orders.append(tuple(order))
    slots = (parts, n, per // parts, width)
    sems = pltpu.SemaphoreType.DMA((parts, levels))
    whole = width * cores
    return pl.pallas_call(
        functools.partial(exchange_kernel, n, tuple(orders)),
        out_shape=(
            jax.ShapeDtypeStruct((per, width), jnp.float32),
            jax.ShapeDtypeStruct((whole, whole), jnp.float32),
        ),
        in_specs=[pl.BlockSpec(memory_space=pltpu.VMEM)],
        out_specs=(pl.BlockSpec(memory_space=pltpu.VMEM),) * 2,
        scratch_shapes=[
            pltpu.VMEM(slots, jnp.float32),
            pltpu.VMEM(slots, jnp.float32),
            pltpu.VMEM((parts, n, per // parts, whole), jnp.float32),
            sems, sems, sems, sems,
            pltpu.SemaphoreType.DMA((parts, levels + 1)),
            pltpu.SemaphoreType.DMA((parts, levels + 1)),
        ],
        compiler_params=pltpu.CompilerParams(
            collective_id=0, has_side_effects=True, vmem_limit_bytes=60 * 1024 * 1024
        ),
    )(outgoing.reshape(n, per, width))


def factor_block(block, inverse):
    size = block.shape[0]
    sub = lax.broadcasted_iota(jnp.int32, (8, size), 0)
    rest_a = block
    rest_b = None
    if inverse:
        rest_b = (
            lax.broadcasted_iota(jnp.int32, (size, size), 0) == lax.broadcasted_iota(jnp.int32, (size, size), 1)
        ).astype(jnp.float32)
    upper, lower = [], []
    for group in range(size // 8):
        first = group * 8
        columns = [jnp.broadcast_to(rest_a[:, first + j : first + j + 1], rest_a.shape) for j in range(8)]
        top_c, rest_c = [c[:8] for c in columns], [c[8:] for c in columns]
        more = first + 8 < size
        top_a, rest_a = rest_a[:8], rest_a[8:]
        if inverse:
            top_b, rest_b = rest_b[:8], rest_b[8:]
        for j in range(8):
            root = lax.rsqrt(top_c[j][j : j + 1])
            top_s = jnp.where(sub > j, top_c[j] * root, 0.0)
            row_a = top_a[j : j + 1] * root
            top_a = jnp.where(sub == j, row_a, top_a - top_s * row_a)
            if more:
                rest_s = rest_c[j] * root
                rest_a = rest_a - rest_s * row_a
            if inverse:
                row_b = top_b[j : j + 1] * root
                top_b = jnp.where(sub == j, row_b, top_b - top_s * row_b)
                if more:
                    rest_b = rest_b - rest_s * row_b
            for later in range(j + 1, 8):
                weight = top_c[later][j : j + 1] * root
                top_c[later] = top_c[later] - top_s * weight
                if more:
                    rest_c[later] = rest_c[later] - rest_s * weight
        upper.append(top_a)
        if inverse:
            lower.append(top_b)
    return jnp.concatenate(upper, axis=0), (jnp.concatenate(lower, axis=0) if inverse else None)


def cholesky_kernel(scale, gram_ref, out_ref, work, upper):
    size = gram_ref.shape[0]
    block = LANES
    work[...] = gram_ref[...] * scale
    upper[...] = jnp.zeros_like(upper)
    triangle = lax.broadcasted_iota(jnp.int32, (block, block), 0) <= lax.broadcasted_iota(
        jnp.int32, (block, block), 1
    )
    dims = (((0,), (0,)), ((), ()))
    for start in range(0, size, block):
        stop = start + block
        last = stop == size
        diagonal, inverse = factor_block(work[start:stop, start:stop], not last)
        upper[start:stop, start:stop] = jnp.where(triangle, diagonal, 0.0)
        if not last:
            panel = jnp.dot(
                inverse, work[start:stop, stop:], precision=HIGHEST, preferred_element_type=jnp.float32
            )
            upper[start:stop, stop:] = panel
            for row in range(stop, size, block):
                work[row : row + block, row:] -= lax.dot_general(
                    panel[:, row - stop : row - stop + block],
                    panel[:, row - stop :],
                    dims,
                    precision=HIGHEST,
                    preferred_element_type=jnp.float32,
                )
    width = out_ref.shape[1]
    out_ref[...] = upper[:, pl.ds(pl.multiple_of(lax.axis_index("cols") * width, width), width)]


def cholesky(gram, scale, width):
    size = gram.shape[0]
    return pl.pallas_call(
        functools.partial(cholesky_kernel, scale),
        out_shape=jax.ShapeDtypeStruct((size, width), jnp.float32),
        in_specs=[pl.BlockSpec(memory_space=pltpu.VMEM)],
        out_specs=pl.BlockSpec(memory_space=pltpu.VMEM),
        scratch_shapes=[pltpu.VMEM((size, size), jnp.float32)] * 2,
    )(gram)


def solution(mesh):
    n, cores = mesh.shape["rows"], mesh.shape["cols"]

    def body(design, signs, kept):
        widths = design.shape[1]
        outgoing = transform(design, signs, kept, design.shape[0] * n)
        sketch, gram = exchange(outgoing, n, cores)
        return (sketch, cholesky(gram, 1.0 / kept.shape[0], widths))

    return jax.shard_map(
        body,
        mesh=mesh,
        in_specs=(P("rows", "cols"), P("rows"), P()),
        out_specs=(P("rows", "cols"), P(None, "cols")),
        check_vma=False,
    )
```

time: 272 us -> 72.7 us (0.27)
  waiting for transfers between devices: 111 us -> 0 us
  other arithmetic: 89.4 us -> 0 us
  Pallas kernels: 0 us -> 70.1 us
  blocking collectives: 36.5 us -> 0 us
  between operations: 16.9 us -> 0.65 us
  local copies, waits for them, and re-layouts: 11 us -> 0.63 us
  matrix products: 6.7 us -> 0 us
    psum x1 -> x0, waiting for transfers between devices: 111 us -> none  [body(): gram = lax.psum(partial_gram, 'rows') / kept_total]
    another operation x14 -> x0, other arithmetic: 78.6 us -> none  [body(): factor = jnp.linalg.cholesky(gram).T]
    pallas_call x0 -> x3, Pallas kernels: none -> 70.1 us  [the longest x1 45.9 us: exchange(): pl.pallas_call(functools.partial(exchange_kernel, n, tuple(orders)), out_...]
    all_to_all x1 -> x0, blocking collectives: 34.5 us -> none  [body(): lax.all_to_all(outgoing, 'rows', split_axis=0, concat_axis=0, tiled=True)]
    mul x8 -> x0, other arithmetic: 7.64 us -> none  [the longest x6 7.1 us: hadamard(): matrix = jnp.kron(matrix, base)]
    mul x8 -> x0, local copies, waits for them, and re-layouts: 5.19 us -> none  [the longest x7 5.12 us: hadamard(): matrix = jnp.kron(matrix, base)]
    dot_general x3 -> x0, matrix products: 4.84 us -> none  [the longest x1 2.06 us: body(): jnp.dot(whole.T, whole, precision=lax.Precision.HIGHEST, preferred_elemen...]
    gather x1 -> x0, local copies, waits for them, and re-layouts: 3.46 us -> none  [signed_rows(): return jnp.take(transformed, offsets, axis=0) * factor[:, None]]
  transfers between devices with their start and end apart: 1 -> 0, of which waited for: 1 -> 0; matrix products, arithmetic and copies ran while one was open for 0% -> 0% of each run, Pallas kernels for 0% -> 0%
where the time goes in v1:
time: 72.7 us; the launch traced here: 71.4 us
  Pallas kernels  70.1 us (96%)
    pallas_call x1, Pallas kernels, exchange(): pl.pallas_call(functools.partial(exchange_kernel, n, tuple(orders)), out_...  45.9 us
    pallas_call x1, Pallas kernels, cholesky(): pl.pallas_call(functools.partial(cholesky_kernel, scale), out_shape=jax.S...  18.8 us
    pallas_call x1, Pallas kernels, transform(): pl.pallas_call(functools.partial(transform_kernel, 1.0 / math.sqrt(total_...  5.37 us

profile of v1, /device:TPU:0, one launch (start us, length us, event | category | flops | bytes accessed | tf_op | source)
XLA Modules:
  0.0 71.4 jit_solution(7067906110913965042)
XLA Ops:
  0.6 5.4 %shard_map.50 = f32[1024,256]{1,0:T(8,128)} custom-call(f32[1024,256]{1,0:T(8,128)} %design_ref.1, s32[8,128]{1,0:T(8,128)} %bitcast.4, s32[8,128]{1,0:T(8,128)} %bitcast.5), custom_call_target="tpu_custom_call" | custom-call | flops 1610612736 | bytes 2097152 | tf_op jit(solution)/shard_map/pallas_call | solution.py:55
  6.0 45.9 %shard_map.51 = (f32[64,256]{1,0:T(8,128)}, f32[512,512]{1,0:T(8,128)}) custom-call(f32[16,64,256]{2,1,0:T(8,128)} %bitcast.3), custom_call_target="tpu_custom_call" | custom-call | tf_op jit(solution)/shard_map/pallas_call | solution.py:210
  51.9 0.0 copy-start
  51.9 18.8 %shard_map.52 = f32[512,256]{1,0:T(8,128)} custom-call(f32[512,512]{1,0:T(8,128)} %get-tuple-element.5.gram_ref), custom_call_target="tpu_custom_call" | custom-call | tf_op jit(solution)/shard_map/pallas_call | solution.py:307
  70.8 0.0 copy-done
  70.8 0.6 copy.6
Async XLA Ops:
  51.9 18.8 %copy-start = (f32[64,256]{1,0:T(8,128)S(1)}, f32[64,256]{1,0:T(8,128)}, u32[]{:S(2)}) copy-start(f32[64,256]{1,0:T(8,128)} %get-tuple-element.8) | copy-start | bytes 196612
